TPU v7x, 256 devices: a whole 4x4x8 slice. The times are simulated.
256 devices in a mesh: gx: 16 (over y, z_lo, core), yz: 16 (over x, z_hi).
Axes of the slice: x: 4, y: 4, z: 8 (z_hi: 4, z_lo: 2; z = z_hi * 2 + z_lo), core: 2. Of those that a mesh axis runs over, the one named last changes fastest.
Arguments:
- fluid_offsets: float32 [3, 16, 48, 64, 128], P(None, None, 'gx', 'yz'), may hold values from 0 to 1
- fluid_velocity: float32 [3, 16, 48, 64, 128], P(None, None, 'gx', 'yz'), may hold values from -6 to 6
- fluid_density: float32 [16, 48, 64, 128], P(None, 'gx', 'yz'), may hold values from 0.97 to 1.03
- fluid_counts: int32 [48, 64, 128], P('gx', 'yz'), may hold values from 0 to 16, as said below
- wall_offsets: float32 [3, 4, 48, 64, 128], P(None, None, 'gx', 'yz'), may hold values from 0 to 1
- wall_counts: int32 [48, 64, 128], P('gx', 'yz'), may hold values from 0 to 4, as said below
Outputs:
- velocity_step: float32 [3, 16, 48, 64, 128], P(None, None, 'gx', 'yz')
- density_rate: float32 [16, 48, 64, 128], P(None, 'gx', 'yz')
Inputs may be any that keep to these rules, and one draw needn't show every extreme that they name: `fluid_counts`: slots 0 to count - 1 of a cell hold fluid particles; cells inside solid obstacles hold none. `wall_counts`: slots 0 to count - 1 of a cell hold wall particles; every cell of the bottom layer (last index 0) holds 4.
All inputs are finite; a program needn't handle non-finite values.
Results may differ from a plain program's by a relative error of at most 0.0003.
Values sent between devices are 32-bit elements; how exact they have to be, the bound alone decides.
No kernel may reach another device: no remote copies, remote signals or barrier semaphores. Data moves between devices by JAX's collectives and lax.ppermute only.
A program may use at most 128 MiB of HBM per device.

v0:
```python
from functools import partial

import jax
import jax.numpy as jnp
import numpy as np
from jax import lax
from jax.experimental import pallas as pl
from jax.experimental.pallas import tpu as pltpu
from jax.sharding import Mesh
from jax.sharding import PartitionSpec as P

GX = ("gx_0", "gx_1", "gx_2")
YZ = ("yz_0", "yz_1")

GRAVITY = 2.0
STIFFNESS = 100.0 / 7.0
SOFT = 0.0025
SCALE = 2.5
FAR = 1.0e6
PAD = -1.0e6
BX, BY, SLOTS, WALLS = 3, 4, 16, 4
COLS = BX * BY
ROWS = 144
WIRE = 128
NEAR = 64
WALL = 112
PART = (0, 16, 32, 48, 128, 64, 80, 96)
F32 = jnp.float32


def rows8(ref, base):
    return ref[pl.ds(pl.multiple_of(base, 8), 8), :]


def spread(ref, row):
    return ref[pl.ds(row, 8, stride=0), :]


def put8(ref, base, value):
    ref[pl.ds(pl.multiple_of(base, 8), 8), :] = value


def lanes():
    return lax.broadcasted_iota(jnp.int32, (8, 128), 1)


def shifted(value, move, fill=None):
    out = pltpu.roll(value, (-move) % 128, 1)
    if fill is None:
        return out
    return jnp.where(lanes() == (127 if move > 0 else 0), fill, out)


def slope(dx, dy, dz):
    squared = dx * dx + dy * dy + dz * dz
    distance = squared * lax.rsqrt(jnp.maximum(squared, 1e-30))
    remain = jnp.maximum(1.0 - distance, 0.0)
    return squared, remain * remain * remain


def weight(dx, dy, dz):
    squared = dx * dx + dy * dy + dz * dz
    distance = squared * lax.rsqrt(jnp.maximum(squared, 1e-30))
    remain = jnp.maximum(1.0 - distance, 0.0)
    twice = remain * remain
    return (twice * twice) * (4.0 * distance + 1.0)


def fluid_pair(t, s):
    dx, dy, dz = t[0] - s[0], t[1] - s[1], t[2] - s[2]
    squared, cube = slope(dx, dy, dz)
    approach = (t[5] - s[5]) * dx + (t[6] - s[6]) * dy + (t[7] - s[7]) * dz
    below = (squared + SOFT) * (t[3] + s[3])
    viscous = jnp.minimum(approach, 0.0) * pl.reciprocal(below, approx=True)
    factor = cube * ((t[4] + s[4]) - viscous)
    return factor * dx, factor * dy, factor * dz, cube * approach


def wall_pair(t, s):
    dx, dy, dz = t[0] - s[0], t[1] - s[1], t[2] - s[2]
    squared, cube = slope(dx, dy, dz)
    approach = t[5] * dx + t[6] * dy + t[7] * dz
    below = (squared + SOFT) * t[3]
    viscous = jnp.minimum(approach, 0.0) * pl.reciprocal(below, approx=True)
    factor = cube * ((t[4] + s[3]) - viscous)
    return factor * dx, factor * dy, factor * dz, cube * approach


def pressure_term(rho):
    rho2 = rho * rho
    return (STIFFNESS * ((rho2 * rho2) * (rho2 * rho) - 1.0)) / rho2


def pack_body(
    off_in, vel_in, den_in, cnt_in, woff_in, wcnt_in, own, right, left, up, down,
    off, vel, den, cnt, woff, wcnt, sems,
):
    copies = [
        pltpu.make_async_copy(src, dst, sems.at[n])
        for n, (src, dst) in enumerate(
            zip((off_in, vel_in, den_in, cnt_in, woff_in, wcnt_in), (off, vel, den, cnt, woff, wcnt))
        )
    ]
    for copy in copies:
        copy.start()
    for copy in copies:
        copy.wait()
    slot = lax.broadcasted_iota(jnp.int32, (SLOTS, 128), 0)
    wslot = lax.broadcasted_iota(jnp.int32, (WALLS, 128), 0)
    for q in range(COLS):
        x, y = divmod(q, BY)
        base = q * ROWS
        live = slot < jnp.broadcast_to(cnt[x, y : y + 1, :], (SLOTS, 128))

        def take(ref, part):
            return ref[pl.ds(part * SLOTS * COLS + q, SLOTS, stride=COLS), :]

        rho = take(den, 0)
        parts = (
            jnp.where(live, take(off, 0) + float(x), FAR),
            take(off, 1) + float(y),
            take(off, 2),
            0.5 * rho,
            pressure_term(rho),
            take(vel, 0),
            take(vel, 1),
            take(vel, 2),
        )
        for at, part in zip(PART, parts):
            own[base + at : base + at + 16, :] = part
        live = wslot < jnp.broadcast_to(wcnt[x, y : y + 1, :], (WALLS, 128))

        def wtake(part):
            return woff[pl.ds(part * WALLS * COLS + q, WALLS, stride=COLS), :]

        base += WALL
        own[base : base + 4, :] = jnp.where(live, wtake(0) + float(x), FAR)
        own[base + 4 : base + 8, :] = wtake(1) + float(y)
        own[base + 8 : base + 12, :] = wtake(2)
        own[base + 12 : base + 16, :] = jnp.where(live, 1.0, 0.0)
    for ref, first in ((right, BX - 1), (left, 0)):
        for y in range(BY):
            base = (first * BY + y) * ROWS
            ref[y * WIRE : (y + 1) * WIRE, :] = own[base : base + WIRE, :]
            base = (1 * BY + y) * ROWS
            start = BY * WIRE + y * NEAR
            ref[start : start + NEAR, :] = own[base : base + NEAR, :]
    for ref, near, next_ in ((up, BY - 1, BY - 2), (down, 0, 1)):
        for x in range(BX):
            base = (x * BY + near) * ROWS
            ref[x * WIRE : (x + 1) * WIRE, :] = own[base : base + WIRE, :]
            base = (x * BY + next_) * ROWS
            start = BX * WIRE + x * NEAR
            ref[start : start + NEAR, :] = own[base : base + NEAR, :]


XMSG = BY * (WIRE + NEAR)
YMSG = BX * (WIRE + NEAR)
CMSG = 2 * WIRE + 6 * NEAR
XHALO = 8 * ROWS + 8 * NEAR


def corner_rows(ring, fx):
    if ring == 1:
        return {-1: 0, 3: WIRE, -2: 2 * WIRE, 4: 2 * WIRE + NEAR}[fx]
    return 2 * WIRE + 2 * NEAR + {-2: 0, -1: 1, 3: 2, 4: 3}[fx] * NEAR


def x_rows(fx, y):
    if fx in (-1, 3):
        return ((0 if fx < 0 else BY) + y) * ROWS
    return 8 * ROWS + ((0 if fx < 0 else BY) + y) * NEAR


def settle(src, base, dst, to, full, axis, move):
    for h in range(2):
        rho = src[base + 48 + 8 * h : base + 56 + 8 * h, :]
        for k in (0, 1, 2, 3, 5, 6, 7) if full else range(4):
            row = PART[k] + 8 * h
            value = src[base + row : base + row + 8, :]
            if k == axis:
                value = value + move
            if k == 0:
                value = jnp.where(rho > 0.0, value, FAR)
            dst[to + row : to + row + 8, :] = value
        if full:
            term = pressure_term(jnp.where(rho > 0.0, 2.0 * rho, 1.0))
            dst[to + 128 + 8 * h : to + 136 + 8 * h, :] = term
    if full:
        base, to = base + WALL, to + WALL
        mask = src[base + 12 : base + 16, :]
        for k in range(3):
            value = src[base + 4 * k : base + 4 * k + 4, :]
            if k == axis:
                value = value + move
            if k == 0:
                value = jnp.where(mask > 0.0, value, FAR)
            dst[to + 4 * k : to + 4 * k + 4, :] = value
        dst[to + 12 : to + 16, :] = mask


def forward_body(own, from_left, from_right, halo, up, down):
    for src, fx, fx2, move in ((from_left, -1, -2, -3.0), (from_right, 3, 4, 3.0)):
        for y in range(BY):
            settle(src, y * WIRE, halo, x_rows(fx, y), True, 0, move)
            settle(src, BY * WIRE + y * NEAR, halo, x_rows(fx2, y), False, 0, move)
    for ref, near, next_ in ((up, BY - 1, BY - 2), (down, 0, 1)):
        for ring, y in ((1, near), (2, next_)):
            for fx in (-2, -1, 3, 4):
                count = WIRE if (ring == 1 and fx in (-1, 3)) else NEAR
                to = corner_rows(ring, fx)
                base = x_rows(fx, y)
                ref[to : to + count, :] = halo[base : base + count, :]


def roll_columns(src, rolled, count):
    for q in range(count):
        for v, move in enumerate((-1, 1)):
            for k in range(8):
                for h in range(2):
                    base = q * ROWS + PART[k] + 8 * h
                    value = shifted(src[base : base + 8, :], move, PAD if k == 0 else None)
                    if k == 2:
                        value = value + float(move)
                    to = (v * count + q) * 128 + 16 * k + 8 * h
                    rolled[to : to + 8, :] = value


def own_body(count, selfs, tab, own, out, rolled, acc, racc):
    zero = jnp.zeros((8, 128), F32)

    def clear(i, c):
        base = i * 128
        for k in range(16):
            put8(acc, base + 8 * k, zero)
        return c

    lax.fori_loop(0, COLS * 4 * SLOTS * 8 // 128, clear, 0)

    def clear_r(i, c):
        for k in range(24):
            put8(racc, i * 192 + 8 * k, zero)
        return c

    lax.fori_loop(0, COLS, clear_r, 0)

    roll_columns(own, rolled, COLS)

    def block(t, s, v, symmetric):
        for h in range(2):
            if v == 0:
                src = [rows8(own, s * ROWS + PART[k] + 8 * h) for k in range(8)]
            else:
                src = [rows8(rolled, ((v - 1) * COLS + s) * 128 + 16 * k + 8 * h) for k in range(8)]
            back = [zero] * 4
            for i in range(SLOTS):
                dst = [spread(own, t * ROWS + PART[k] + i) for k in range(8)]
                terms = fluid_pair(dst, src)
                for c in range(4):
                    base = ((t * 4 + c) * SLOTS + i) * 8
                    put8(acc, base, rows8(acc, base) + terms[c])
                if symmetric:
                    for c in range(3):
                        back[c] = back[c] - terms[c]
                    back[3] = back[3] + terms[3]
            if symmetric:
                for c in range(4):
                    base = (s * 3 + v) * 64 + 16 * c + 8 * h
                    put8(racc, base, rows8(racc, base) + back[c])

    def pair(e, c):
        t, s = tab[0, e], tab[1, e]
        for v in range(3):
            block(t, s, v, True)
        return c

    lax.fori_loop(0, count, pair, 0)
    if selfs:

        def alone(q, c):
            block(q, q, 0, False)
            block(q, q, 2, True)
            return c

        lax.fori_loop(0, COLS, alone, 0)

    sub = lax.broadcasted_iota(jnp.int32, (8, 128), 0)

    def gather_rows(values):
        for bit in (1, 2, 4):
            odd = (sub & bit) != 0
            values = [
                jnp.where(odd, b, a) + pltpu.roll(jnp.where(odd, a, b), bit, 0) if bit == 4
                else jnp.where(odd, b + pltpu.roll(b, bit, 0), a + pltpu.roll(a, 8 - bit, 0))
                for a, b in zip(values[0::2], values[1::2])
            ]
        return values[0]

    def finish(group, c):
        for n in range(3):
            q = group * 3 + n
            for k in range(8):
                start = (q * 4 * SLOTS + 8 * k) * 8
                value = gather_rows([rows8(acc, start + 8 * i) for i in range(8)])
                value = value + rows8(racc, q * 192 + 8 * k)
                value = value + pltpu.roll(rows8(racc, q * 192 + 64 + 8 * k), 127, 1)
                value = value + pltpu.roll(rows8(racc, q * 192 + 128 + 8 * k), 1, 1)
                put8(out, q * 64 + 8 * k, value)
        return c

    lax.fori_loop(0, COLS // 3, finish, 0)


SIDES = (
    [(-1, y) for y in range(BY)]
    + [(BX, y) for y in range(BY)]
    + [(x, -1) for x in range(BX)]
    + [(x, BY) for x in range(BX)]
)
CORNERS = [(-1, -1), (BX, -1), (-1, BY), (BX, BY)]
FRAME = (BX + 4) * (BY + 4)
LOW = 16
ROOM = 64500000
MOVES = [(sx, sy) for sx in (-1, 0, 1) for sy in (-1, 0, 1)]


def frame(fx, fy):
    return (fx + 2) * 8 + fy + 2


def turn(value, shift):
    return pltpu.roll(value, shift % 128, 1) if shift % 128 else value


def against(own, q, h, sources, total, first=0, last=SLOTS):
    t = [rows8(own, q * ROWS + PART[k] + 8 * h) for k in range(8)]
    sums = [jnp.zeros((8, 128), F32)] * 4
    for ref, base, at in sources:
        for j in range(first, last):
            terms = fluid_pair(t, [spread(ref, base + at[k] + j) for k in range(8)])
            sums = [a + b for a, b in zip(sums, terms)]
    for c in range(4):
        base = q * 64 + 16 * c + 8 * h
        put8(total, base, rows8(total, base) + sums[c])


DENSE = tuple(16 * k for k in range(8))


def crowded(refs):
    least = jnp.full((8, 128), FAR, F32)
    for ref, base in refs:
        least = jnp.minimum(least, ref[base + 8 : base + 16, :])
    return jnp.min(least) < 0.5 * FAR


def sides_body(count, tab, own, halo, from_down, from_up, inner, near, total, rolled):
    for n, (fx, fy) in enumerate(SIDES):
        if 0 <= fy < BY:
            base = x_rows(fx, fy)
            near[n * ROWS : (n + 1) * ROWS, :] = halo[base : base + ROWS, :]
        else:
            src, move = (from_down, -4.0) if fy < 0 else (from_up, 4.0)
            settle(src, fx * WIRE, near, n * ROWS, True, 1, move)
    total[...] = inner[...]
    roll_columns(near, rolled, len(SIDES))
    many_own = crowded([(own, q * ROWS) for q in range(COLS)])
    many_near = crowded([(near, n * ROWS) for n in range(len(SIDES))])

    def pair(e, carry):
        q, n = tab[0, e], tab[1, e]
        sources = [(near, n * ROWS, PART)]
        sources += [(rolled, (v * len(SIDES) + n) * 128, DENSE) for v in range(2)]
        against(own, q, 0, sources, total, 0, 8)

        @pl.when(many_near)
        def _():
            against(own, q, 0, sources, total, 8, 16)

        @pl.when(many_own)
        def _():
            against(own, q, 1, sources, total, 0, 8)

        @pl.when(many_own & many_near)
        def _():
            against(own, q, 1, sources, total, 8, 16)

        return carry

    lax.fori_loop(0, count, pair, 0)


def sum_walls(spots, sources):
    zero = jnp.zeros((8, 128), F32)
    mass, load = [zero] * WALLS, [zero] * WALLS
    for get in sources:
        s = get()
        for w in range(WALLS):
            dz = spots[w][2] - s[2]
            value = weight(spots[w][0] - s[0], spots[w][1] - s[1], dz)
            mass[w] = mass[w] + value
            load[w] = load[w] + value * (s[4] - s[3] * dz)
    return [
        jnp.sum(load[w], axis=0, keepdims=True) / jnp.maximum(jnp.sum(mass[w], axis=0, keepdims=True), 1.0)
        for w in range(WALLS)
    ]


def rim_body(
    own, halo, near, down_side, up_side, down_corner, up_corner, part, acc_out, rate_out, top,
    corner, rolled, geo, walls, low_walls, total, bottom, target, wbot, wroll, rbot, stage,
    low_geo, low_wall, low_target, low_sum,
):
    zero = jnp.zeros((8, 128), F32)
    lane = lanes()
    sub = lax.broadcasted_iota(jnp.int32, (8, 128), 0)
    for n, (fx, fy) in enumerate(CORNERS):
        src, move = (down_corner, -4.0) if fy < 0 else (up_corner, 4.0)
        settle(src, corner_rows(1, fx), corner, n * ROWS, True, 1, move)
    total[...] = part[...]
    roll_columns(corner, rolled, len(CORNERS))
    for n, (fx, fy) in enumerate(CORNERS):
        q = min(max(fx, 0), BX - 1) * BY + min(max(fy, 0), BY - 1)
        sources = [(corner, n * ROWS, PART)]
        sources += [(rolled, (v * len(CORNERS) + n) * 128, DENSE) for v in range(2)]
        for h in range(2):
            against(own, q, h, sources, total)

    def place(fx, fy):
        if 0 <= fx < BX and 0 <= fy < BY:
            return own, (fx * BY + fy) * ROWS
        if (fx, fy) in SIDES:
            return near, SIDES.index((fx, fy)) * ROWS
        return corner, CORNERS.index((fx, fy)) * ROWS

    for fx in range(-2, BX + 2):
        for fy in range(-2, BY + 2):
            to = frame(fx, fy) * 80
            if -1 <= fx <= BX and -1 <= fy <= BY:
                ref, base = place(fx, fy)
            elif 0 <= fy < BY:
                ref, base = halo, x_rows(fx, fy)
            else:
                ring = 2 if fy in (-2, BY + 1) else 1
                move = -4.0 if fy < 0 else 4.0
                if 0 <= fx < BX:
                    src, base = (down_side if fy < 0 else up_side), BX * WIRE + fx * NEAR
                else:
                    src, base = (down_corner if fy < 0 else up_corner), corner_rows(ring, fx)
                settle(src, base, geo, to, False, 1, move)
                ref, base = geo, to
            for h in range(2):
                rho = 2.0 * ref[base + 48 + 8 * h : base + 56 + 8 * h, :]
                if ref is not geo:
                    for k in range(3):
                        row = 16 * k + 8 * h
                        geo[to + row : to + row + 8, :] = ref[base + row : base + row + 8, :]
                rho2 = rho * rho
                geo[to + 48 + 8 * h : to + 56 + 8 * h, :] = GRAVITY * rho
                geo[to + 64 + 8 * h : to + 72 + 8 * h, :] = STIFFNESS * ((rho2 * rho2) * (rho2 * rho) - 1.0)

    for k in range(10):
        low, high = zero, zero
        for h in range(FRAME):
            value = geo[h * 80 + 8 * k : h * 80 + 8 * k + 8, :]
            low = jnp.where(lane == h, turn(value, h), low)
            high = jnp.where(lane == h, turn(value, h - 1), high)
        bottom[8 * k : 8 * k + 8, :] = low
        bottom[80 + 8 * k : 88 + 8 * k, :] = high + 1.0 if k in (4, 5) else high
    for k in range(16):
        low, high = zero, zero
        for q in range(COLS):
            h = frame(*divmod(q, BY))
            base = q * ROWS + PART[k // 2] + 8 * (k % 2)
            value = own[base : base + 8, :]
            low = jnp.where(lane == h, turn(value, h), low)
            high = jnp.where(lane == h, turn(value, h - 1), high)
        target[8 * k : 8 * k + 8, :] = low
        target[128 + 8 * k : 136 + 8 * k, :] = high + 1.0 if k in (4, 5) else high
    codes = [zero] * 4
    wa, wb = zero, zero
    for n in range(30):
        fx, fy = n // 6 - 1, n % 6 - 1
        ref, base = place(fx, fy)
        base += WALL
        xy, zm = ref[base : base + 8, :], ref[base + 8 : base + 16, :]
        h = frame(fx, fy)
        wa = jnp.where(lane == h, turn(xy, h), wa)
        wb = jnp.where(lane == h, turn(zm, h), wb)
        mask = jnp.max(jnp.where(sub >= 4, zm, 0.0), axis=0, keepdims=True)
        one = lane[0:1]
        high = jnp.max(jnp.where(one >= LOW - 1, mask, 0.0), axis=1, keepdims=True)
        some = jnp.max(jnp.where((one >= 1) & (one < LOW - 1), mask, 0.0), axis=1, keepdims=True)
        some = jnp.where(high > 0.0, 0.0, some)
        bit = float(1 << (n % 15))
        g = 0 if n < 15 else 1
        codes[g] = codes[g] + jnp.where(high > 0.0, bit, 0.0)
        codes[2] = jnp.maximum(codes[2], some)
        walls[n * 16 : n * 16 + 8, :] = jnp.where((lane == 0) & (sub < 4), FAR, xy)
        walls[n * 16 + 8 : n * 16 + 16, :] = zm
        keep = jnp.broadcast_to(some > 0.0, (8, 128)) & (lane >= 1) & (lane < LOW - 1)
        low_walls[n * 8 : n * 8 + 8, :] = jnp.where((sub >= 4) | keep, xy, FAR)
    wbot[0:8, :] = wa
    wbot[8:16, :] = wb
    flags_a = jnp.max(codes[0]).astype(jnp.int32)
    flags_b = jnp.max(codes[1]).astype(jnp.int32)
    low_any = jnp.max(codes[2]) > 0.0

    def from_bottom(z, h, back):
        def get():
            base = 80 * z + 8 * h
            return [turn(bottom[base + 16 * k : base + 16 * k + 8, :], back) for k in range(5)]

        return get

    spots = [[spread(wbot, 4 * k + w) for k in range(3)] for w in range(WALLS)]
    found = sum_walls(spots, [from_bottom(z, h, -(sx * 8 + sy)) for sx, sy in MOVES for z in range(2) for h in range(2)])
    for w in range(WALLS):
        wbot[12 + w : 13 + w, :] = found[w]
    for m, (sx, sy) in enumerate(MOVES):
        for k in range(2):
            wroll[16 * m + 8 * k : 16 * m + 8 * k + 8, :] = turn(wbot[8 * k : 8 * k + 8, :], -(sx * 8 + sy))
    for z in range(2):
        for h in range(2):
            t = [target[128 * z + 16 * k + 8 * h : 128 * z + 16 * k + 8 * h + 8, :] for k in range(8)]
            t[3] = t[3] + 0.5
            sums = [zero] * 4
            for m in range(9):
                for w in range(WALLS):
                    terms = wall_pair(t, [spread(wroll, 16 * m + 4 * k + w) for k in range(4)])
                    sums = [a + b for a, b in zip(sums, terms)]
            for c in range(4):
                rbot[64 * z + 16 * c + 8 * h : 64 * z + 16 * c + 8 * h + 8, :] = sums[c]
    for q in range(COLS):
        h = frame(*divmod(q, BY))
        for k in range(8):
            base = q * 64 + 8 * k
            low = turn(rbot[8 * k : 8 * k + 8, :], -h)
            high = turn(rbot[64 + 8 * k : 72 + 8 * k, :], 1 - h)
            add = jnp.where(lane == 0, low, jnp.where(lane == 1, high, 0.0))
            total[base : base + 8, :] = total[base : base + 8, :] + add

    @pl.when(low_any)
    def _():
        block = lane // LOW
        for i in range(BX + 4):
            for k in range(10):
                value = zero
                for j in range(8):
                    base = (i * 8 + j) * 80 + 8 * k
                    value = jnp.where(block == j, turn(geo[base : base + 8, :], j * LOW), value)
                low_geo[i * 80 + 8 * k : i * 80 + 8 * k + 8, :] = value
        for i in range(BX + 2):
            xy, zm = jnp.where(sub < 4, FAR, zero), zero
            for j in range(6):
                n = i * 6 + j
                xy = jnp.where(block == j + 1, turn(low_walls[n * 8 : n * 8 + 8, :], (j + 1) * LOW), xy)
                zm = jnp.where(block == j + 1, turn(walls[n * 16 + 8 : n * 16 + 16, :], (j + 1) * LOW), zm)
            low_wall[i * 16 : i * 16 + 8, :] = xy
            low_wall[i * 16 + 8 : i * 16 + 16, :] = zm
        for i in range(BX):
            for k in range(16):
                value = zero
                for j in range(BY):
                    base = (i * BY + j) * ROWS + PART[k // 2] + 8 * (k % 2)
                    value = jnp.where(block == j + 2, turn(own[base : base + 8, :], (j + 2) * LOW), value)
                low_target[i * 128 + 8 * k : i * 128 + 8 * k + 8, :] = value
        steps = [(sx, sy, dz) for sx, sy in MOVES for dz in (-1, 0, 1)]

        def press(i, carry):
            for m, (sx, sy, dz) in enumerate(steps):
                for k in range(10):
                    value = turn(rows8(low_geo, (i + 1 + sx) * 80 + 8 * k), -(sy * LOW + dz))
                    if k in (4, 5) and dz:
                        value = value + float(dz)
                    stage[m * 80 + 8 * k : m * 80 + 8 * k + 8, :] = value

            def from_stage(m, h):
                return lambda: [stage[m * 80 + 16 * k + 8 * h : m * 80 + 16 * k + 8 * h + 8, :] for k in range(5)]

            spots = [[spread(low_wall, i * 16 + 4 * k + w) for k in range(3)] for w in range(WALLS)]
            found = sum_walls(spots, [from_stage(m, h) for m in range(27) for h in range(2)])
            for w in range(WALLS):
                low_wall[pl.ds(i * 16 + 12 + w, 1), :] = found[w]
            return carry

        lax.fori_loop(0, BX + 2, press, 0)

        def push(i, carry):
            for m, (sx, sy, dz) in enumerate(steps):
                for k in range(2):
                    value = turn(rows8(low_wall, (i + 1 + sx) * 16 + 8 * k), -(sy * LOW + dz))
                    if k == 1 and dz:
                        value = jnp.where(sub < 4, value + float(dz), value)
                    stage[m * 16 + 8 * k : m * 16 + 8 * k + 8, :] = value
            for h in range(2):
                t = [rows8(low_target, i * 128 + 16 * k + 8 * h) for k in range(8)]
                t[3] = t[3] + 0.5
                sums = [zero] * 4
                for m in range(27):
                    for w in range(WALLS):
                        terms = wall_pair(t, [spread(stage, 16 * m + 4 * k + w) for k in range(4)])
                        sums = [a + b for a, b in zip(sums, terms)]
                for c in range(4):
                    put8(low_sum, i * 64 + 16 * c + 8 * h, sums[c])
            return carry

        lax.fori_loop(0, BX, push, 0)
        for i in range(BX):
            for j in range(BY):
                for k in range(8):
                    base = (i * BY + j) * 64 + 8 * k
                    add = turn(low_sum[i * 64 + 8 * k : i * 64 + 8 * k + 8, :], -(j + 2) * LOW)
                    total[base : base + 8, :] = total[base : base + 8, :] + jnp.where(lane < LOW, add, 0.0)

    def wall_column(n, carry):
        flag = jnp.where(n < 15, flags_a >> jnp.minimum(n, 15), flags_b >> jnp.maximum(n - 15, 0)) & 1

        @pl.when(flag == 1)
        def _():
            kx, ky = n // 6, n % 6
            for m, (sx, sy) in enumerate(MOVES):
                h = (kx + 1 + sx) * 8 + ky + 1 + sy
                for k in range(10):
                    value = rows8(geo, h * 80 + 8 * k)
                    for v, move in enumerate((-1, 1)):
                        moved = shifted(value, move, PAD if k < 2 else None)
                        if k in (4, 5):
                            moved = moved + float(move)
                        stage[(v * 9 + m) * 80 + 8 * k : (v * 9 + m) * 80 + 8 * k + 8, :] = moved

            def from_stage(m, v, j):
                def get():
                    if v == 0:
                        h = (kx + 1 + MOVES[m][0]) * 8 + ky + 1 + MOVES[m][1]
                        return [rows8(geo, h * 80 + 16 * k + 8 * j) for k in range(5)]
                    base = ((v - 1) * 9 + m) * 80 + 8 * j
                    return [stage[base + 16 * k : base + 16 * k + 8, :] for k in range(5)]

                return get

            spots = [[spread(walls, n * 16 + 4 * k + w) for k in range(3)] for w in range(WALLS)]
            found = sum_walls(spots, [from_stage(m, v, j) for m in range(9) for v in range(3) for j in range(2)])
            for w in range(WALLS):
                walls[pl.ds(n * 16 + 12 + w, 1), :] = found[w]
            for v, move in enumerate((0, -1, 1)):
                for k in range(2):
                    value = rows8(walls, n * 16 + 8 * k)
                    if move:
                        moved = turn(value, -move)
                        if k == 0:
                            edge = lane == (127 if move > 0 else 0)
                            value = jnp.where(edge & (sub < 4), FAR, moved)
                        else:
                            value = jnp.where(sub < 4, moved + float(move), moved)
                    stage[v * 16 + 8 * k : v * 16 + 8 * k + 8, :] = value

            def over_x(x, c):
                def over_y(y, c):
                    q = x * BY + y
                    for h in range(2):
                        t = [rows8(own, q * ROWS + PART[k] + 8 * h) for k in range(8)]
                        t[3] = t[3] + 0.5
                        sums = [zero] * 4
                        for v in range(3):
                            for w in range(WALLS):
                                terms = wall_pair(t, [spread(stage, v * 16 + 4 * k + w) for k in range(4)])
                                sums = [a + b for a, b in zip(sums, terms)]
                        for c4 in range(4):
                            base = q * 64 + 16 * c4 + 8 * h
                            put8(total, base, rows8(total, base) + sums[c4])
                    return c

                return lax.fori_loop(jnp.maximum(ky - 2, 0), jnp.minimum(ky, BY - 1) + 1, over_y, c)

            lax.fori_loop(jnp.maximum(kx - 2, 0), jnp.minimum(kx, BX - 1) + 1, over_x, 0)

        return carry

    @pl.when(flags_a + flags_b > 0)
    def _():
        lax.fori_loop(0, 30, wall_column, 0)

    most = jnp.zeros((SLOTS, 128), F32)
    for q in range(COLS):
        live = own[q * ROWS : q * ROWS + 16, :] < 0.5 * FAR
        sq = jnp.zeros((SLOTS, 128), F32)
        for c in range(3):
            value = SCALE * total[q * 64 + 16 * c : q * 64 + 16 * c + 16, :]
            if c == 2:
                value = value - GRAVITY
            value = jnp.where(live, value, 0.0)
            sq = sq + value * value
            acc_out[pl.ds(c * SLOTS * COLS + q, SLOTS, stride=COLS), :] = value
        most = jnp.maximum(most, sq)
        rate = -SCALE * total[q * 64 + 48 : q * 64 + 64, :]
        rate_out[pl.ds(q, SLOTS, stride=COLS), :] = jnp.where(live, rate, 0.0)
    top[...] = jnp.zeros(top.shape, F32) + jnp.max(most)


def shape(*dims):
    return jax.ShapeDtypeStruct(dims, F32)


def vmem(rows):
    return pltpu.VMEM((rows, 128), F32)


def call(body, outs, operands, scratch=(), flops=0, tables=0, name=None, space=pltpu.VMEM, room=48 << 20):
    specs = [pl.BlockSpec(memory_space=pltpu.SMEM)] * tables
    specs += [pl.BlockSpec(memory_space=space)] * (len(operands) - tables)
    return pl.pallas_call(
        body,
        out_shape=outs,
        in_specs=specs,
        out_specs=jax.tree.map(lambda _: pl.BlockSpec(memory_space=pltpu.VMEM), outs),
        scratch_shapes=list(scratch),
        cost_estimate=pl.CostEstimate(flops=flops, transcendentals=0, bytes_accessed=1000000),
        compiler_params=pltpu.CompilerParams(vmem_limit_bytes=room),
        name=name,
    )(*operands)


def tables():
    inner, outer = [], []
    for q in range(COLS):
        x, y = divmod(q, BY)
        for sx, sy in MOVES:
            nx, ny = x + sx, y + sy
            if 0 <= nx < BX and 0 <= ny < BY:
                if nx * BY + ny > q:
                    inner.append((q, nx * BY + ny))
            elif (nx, ny) in SIDES:
                outer.append((q, SIDES.index((nx, ny))))
    return np.array(inner, np.int32).T.copy(), np.array(outer, np.int32).T.copy()


def on_device(fluid_offsets, fluid_velocity, fluid_density, fluid_counts, wall_offsets, wall_counts):
    flat = lambda a: a.reshape(-1, 128)
    inner, outer = tables()
    inner_table, outer_table = jnp.asarray(inner), jnp.asarray(outer)
    counts = pltpu.VMEM((BX, BY, 128), jnp.int32)
    own, right, left, up, down = call(
        pack_body,
        (shape(COLS * ROWS, 128), shape(XMSG, 128), shape(XMSG, 128), shape(YMSG, 128), shape(YMSG, 128)),
        (flat(fluid_offsets), flat(fluid_velocity), flat(fluid_density), fluid_counts, flat(wall_offsets), wall_counts),
        (vmem(576), vmem(576), vmem(192), counts, vmem(144), counts, pltpu.SemaphoreType.DMA((6,))),
        space=pltpu.HBM, room=ROOM, name="pack",
    )

    def ring(axis, step):
        size = lax.axis_size(axis)
        return [(i, i + step) for i in range(size) if 0 <= i + step < size]

    def exchange(axis, onward, backward):
        return lax.ppermute(onward, axis, ring(axis, 1)), lax.ppermute(backward, axis, ring(axis, -1))

    down_side, up_side = exchange(YZ, up, down)
    from_left, from_right = exchange(GX, right, left)
    part = call(
        partial(own_body, inner.shape[1], True), shape(COLS * 64, 128), (inner_table, own),
        (vmem(2 * COLS * 128), vmem(COLS * 4 * SLOTS * 8), vmem(COLS * 3 * 64)),
        flops=60000000, tables=1, name="inner",
    )
    down_side, up_side, from_left, from_right, part = lax.optimization_barrier(
        (down_side, up_side, from_left, from_right, part)
    )
    halo, corner_up, corner_down = call(
        forward_body, (shape(XHALO, 128), shape(CMSG, 128), shape(CMSG, 128)),
        (own, from_left, from_right), name="forward",
    )
    down_corner, up_corner = exchange(YZ, corner_up, corner_down)
    near, part = call(
        partial(sides_body, outer.shape[1]), (shape(len(SIDES) * ROWS, 128), shape(COLS * 64, 128)),
        (outer_table, own, halo, down_side, up_side, part), (vmem(2 * len(SIDES) * 128),),
        flops=60000000, tables=1, name="sides",
    )
    part, down_corner, up_corner = lax.optimization_barrier((part, down_corner, up_corner))
    acc, rate, top = call(
        rim_body,
        (shape(3 * SLOTS * COLS, 128), shape(SLOTS * COLS, 128), shape(8, 128)),
        (own, halo, near, down_side, up_side, down_corner, up_corner, part),
        (
            vmem(4 * ROWS), vmem(2 * 4 * 128), vmem(FRAME * 80), vmem(30 * 16), vmem(30 * 8), vmem(COLS * 64),
            vmem(160), vmem(256), vmem(16), vmem(144), vmem(128), vmem(27 * 80),
            vmem(7 * 80), vmem(5 * 16), vmem(3 * 128), vmem(3 * 64),
        ),
        name="rim",
    )
    devices = lax.axis_size(GX + YZ)
    tops = lax.all_to_all(jnp.broadcast_to(top[:1][None], (devices, 1, 128)), GX + YZ, 0, 0, tiled=True)
    largest = jnp.max(tops)
    step = 0.25 * jnp.sqrt(0.5 / (jnp.sqrt(largest) + 1e-6))
    return step * acc.reshape(fluid_offsets.shape), rate.reshape(fluid_density.shape)


def solution(mesh):
    gx, yz = GX, YZ
    split = Mesh(mesh.devices.reshape(4, 2, 2, 4, 4), GX + YZ)
    placed = (
        P(None, None, gx, yz, None),
        P(None, None, gx, yz, None),
        P(None, gx, yz, None),
        P(gx, yz, None),
        P(None, None, gx, yz, None),
        P(gx, yz, None),
    )
    return jax.shard_map(
        on_device,
        mesh=split,
        in_specs=placed,
        out_specs=(P(None, None, gx, yz, None), P(None, gx, yz, None)),
        check_vma=False,
    )
```

profile of v0, /device:TPU:1, one launch (start us, length us, event | category | flops | bytes accessed | tf_op | source)
XLA Modules:
  0.0 113.6 jit_solution(8997738088018018244)
XLA Ops:
  0.6 2.6 %pack.1 = (f32[1728,128]{1,0:T(8,128)}, f32[768,128]{1,0:T(8,128)}, f32[768,128]{1,0:T(8,128)}, f32[576,128]{1,0:T(8,128)}, f32[576,128]{1,0:T(8,128)}) custom-call(f32[576,128]{1,0:T(8,128)} %bitcast.10, f32[576,128]{1,0:T(8,128)} %bitcast.11, f32[192,128]{1,0:T(8,128)} %bitcast.13, s32[3,4,128]{2,1,0:T(4,128)} %cnt_in.1, f32[144,128]{1,0:T(8,128)} %bitcast.14, ...), custom_call_target="tpu_custom_call" | custom-call | bytes 1000000 | tf_op jit(solution)/shard_map/pack/pallas_call | solution.py:712
  3.2 4.9 %collective-permute-start.2 = (f32[768,128]{1,0:T(8,128)}, f32[768,128]{1,0:T(8,128)S(1)}, u32[]{:S(2)}, u32[]{:S(2)}) collective-permute-start(f32[768,128]{1,0:T(8,128)} %get-tuple-element.26), channel_id=1, source_target_pairs={{0,16},{16,32},{32,48},{48,64},{64,80},{80,96},{96,112},{112,128},... | collective-permute-start | bytes 1179656 | tf_op jit(solution)/shard_map/ppermute | solution.py:756
  8.2 1.9 %collective-permute-start.3 = (f32[768,128]{1,0:T(8,128)}, f32[768,128]{1,0:T(8,128)S(1)}, u32[]{:S(2)}, u32[]{:S(2)}) collective-permute-start(f32[768,128]{1,0:T(8,128)} %get-tuple-element.27), channel_id=1, source_target_pairs={{16,0},{32,16},{48,32},{64,48},{80,64},{96,80},{112,96},{128,112},... | collective-permute-start | bytes 1179656 | tf_op jit(solution)/shard_map/ppermute | solution.py:756
  10.1 4.9 %collective-permute-start = (f32[576,128]{1,0:T(8,128)}, f32[576,128]{1,0:T(8,128)S(1)}, u32[]{:S(2)}, u32[]{:S(2)}) collective-permute-start(f32[576,128]{1,0:T(8,128)} %get-tuple-element.24), channel_id=1, source_target_pairs={{0,1},{1,2},{2,3},{3,4},{4,5},{5,6},{6,7},{7,8},{8,9},{9,10},{10,1... | collective-permute-start | bytes 884744 | tf_op jit(solution)/shard_map/ppermute | solution.py:756
  15.0 0.0 copy-start.2
  15.0 1.3 %collective-permute-start.1 = (f32[576,128]{1,0:T(8,128)}, f32[576,128]{1,0:T(8,128)S(1)}, u32[]{:S(2)}, u32[]{:S(2)}) collective-permute-start(f32[576,128]{1,0:T(8,128)} %get-tuple-element.25), channel_id=1, source_target_pairs={{1,0},{2,1},{3,2},{4,3},{5,4},{6,5},{7,6},{8,7},{9,8},{10,9},{11,1... | collective-permute-start | bytes 884744 | tf_op jit(solution)/shard_map/ppermute | solution.py:756
  16.3 0.0 copy-done.2
  16.3 0.0 copy-start
  16.3 1.2 %copy-done = f32[1728,128]{1,0:T(8,128)S(1)} copy-done((f32[1728,128]{1,0:T(8,128)S(1)}, f32[1728,128]{1,0:T(8,128)}, u32[]{:S(2)}) %copy-start) | copy-done | bytes 884760
  17.5 23.5 %inner.1 = f32[768,128]{1,0:T(8,128)S(1)} custom-call(s32[2,29]{1,0:T(2,128)S(1)} %copy-done.2, f32[1728,128]{1,0:T(8,128)S(1)} %copy-done), custom_call_target="tpu_custom_call" | custom-call | flops 60000000 | bytes 1000000 | tf_op jit(solution)/shard_map/inner/pallas_call | solution.py:712
  41.0 0.0 collective-permute-done.from_down.down_side
  41.0 0.0 collective-permute-done.1.from_up.up_side
  41.0 0.0 collective-permute-done.2.from_left
  41.0 0.0 collective-permute-done.3.from_right
  41.1 0.1 forward.1
  41.2 5.8 %collective-permute-start.4 = (f32[640,128]{1,0:T(8,128)S(1)}, f32[640,128]{1,0:T(8,128)S(1)}, u32[]{:S(2)}, u32[]{:S(2)}) collective-permute-start(f32[640,128]{1,0:T(8,128)S(1)} %get-tuple-element.36), channel_id=1, source_target_pairs={{0,1},{1,2},{2,3},{3,4},{4,5},{5,6},{6,7},{7,8},{8,9},{9,10},{10,1... | collective-permute-start | bytes 983048 | tf_op jit(solution)/shard_map/ppermute | solution.py:756
  47.0 0.0 copy-start.1
  47.0 1.3 %collective-permute-start.5 = (f32[640,128]{1,0:T(8,128)S(1)}, f32[640,128]{1,0:T(8,128)S(1)}, u32[]{:S(2)}, u32[]{:S(2)}) collective-permute-start(f32[640,128]{1,0:T(8,128)S(1)} %get-tuple-element.37), channel_id=1, source_target_pairs={{1,0},{2,1},{3,2},{4,3},{5,4},{6,5},{7,6},{8,7},{9,8},{10,9},{11,1... | collective-permute-start | bytes 983048 | tf_op jit(solution)/shard_map/ppermute | solution.py:756
  48.3 0.0 copy-done.1
  48.3 6.6 %sides.1 = (f32[2016,128]{1,0:T(8,128)S(1)}, f32[768,128]{1,0:T(8,128)S(1)}) custom-call(s32[2,34]{1,0:T(2,128)S(1)} %copy-done.1, f32[1728,128]{1,0:T(8,128)S(1)} %copy-done, f32[1664,128]{1,0:T(8,128)S(1)} %get-tuple-element.30.halo, f32[576,128]{1,0:T(8,128)S(1)} %collective-permute-done.from_down.down_side, ...), custom_call_target="tpu_custom_call" | custom-call | flops 60000000 | bytes 1000000 | tf_op jit(solution)/shard_map/sides/pallas_call | solution.py:712
  54.9 0.0 collective-permute-done.4.down_corner
  54.9 12.2 %collective-permute-done.5.up_corner = f32[640,128]{1,0:T(8,128)S(1)} collective-permute-done((f32[640,128]{1,0:T(8,128)S(1)}, f32[640,128]{1,0:T(8,128)S(1)}, u32[]{:S(2)}, u32[]{:S(2)}) %collective-permute-start.5) | collective-permute-done | bytes 327712 | tf_op jit(solution)/shard_map/ppermute | solution.py:756
  67.1 12.5 %rim.1 = (f32[576,128]{1,0:T(8,128)S(1)}, f32[192,128]{1,0:T(8,128)}, f32[8,128]{1,0:T(8,128)S(1)}) custom-call(f32[1728,128]{1,0:T(8,128)S(1)} %copy-done, f32[1664,128]{1,0:T(8,128)S(1)} %get-tuple-element.30.halo, f32[2016,128]{1,0:T(8,128)S(1)} %get-tuple-element.34.near, f32[576,128]{1,0:T(8,128)S(1)} %collective-permute-done.from_down.down_side, ...), custom_call_target="tpu_custom_call" | custom-call | bytes 1000000 | tf_op jit(solution)/shard_map/rim/pallas_call | solution.py:712
  79.6 0.1 broadcast_in_dim.9
  79.7 31.8 %all_to_all.5 = f32[256,1,128]{2,1,0:T(1,128)S(1)} all-to-all(f32[256,1,128]{2,1,0:T(1,128)S(1)} %broadcast_in_dim.9), channel_id=1, replica_groups=mesh['gx_0'=4,'gx_1'=2,'gx_2'=2,'yz_0'=4,'yz_1'=4] {'gx_0','gx_1','gx_2'..., dimensions={0} | all-to-all | bytes 262144 | tf_op jit(solution)/shard_map/all_to_all | solution.py:791
  111.5 0.6 reduce_max.9
  112.9 0.7 broadcast_multiply_fusion
  (1 shorter events, 0.0 us)
Async XLA Ops:
  3.2 37.8 %collective-permute-start.2 = (f32[768,128]{1,0:T(8,128)}, f32[768,128]{1,0:T(8,128)S(1)}, u32[]{:S(2)}, u32[]{:S(2)}) collective-permute-start(f32[768,128]{1,0:T(8,128)} %get-tuple-element.26), channel_id=1, source_target_pairs={{0,16},{16,32},{32,48},{48,64},{64,80},{80,96},{96,112},{112,128},... | collective-permute-start | bytes 1179656 | tf_op jit(solution)/shard_map/ppermute | solution.py:756
  8.2 32.9 %collective-permute-start.3 = (f32[768,128]{1,0:T(8,128)}, f32[768,128]{1,0:T(8,128)S(1)}, u32[]{:S(2)}, u32[]{:S(2)}) collective-permute-start(f32[768,128]{1,0:T(8,128)} %get-tuple-element.27), channel_id=1, source_target_pairs={{16,0},{32,16},{48,32},{64,48},{80,64},{96,80},{112,96},{128,112},... | collective-permute-start | bytes 1179656 | tf_op jit(solution)/shard_map/ppermute | solution.py:756
  10.1 30.9 %collective-permute-start = (f32[576,128]{1,0:T(8,128)}, f32[576,128]{1,0:T(8,128)S(1)}, u32[]{:S(2)}, u32[]{:S(2)}) collective-permute-start(f32[576,128]{1,0:T(8,128)} %get-tuple-element.24), channel_id=1, source_target_pairs={{0,1},{1,2},{2,3},{3,4},{4,5},{5,6},{6,7},{7,8},{8,9},{9,10},{10,1... | collective-permute-start | bytes 884744 | tf_op jit(solution)/shard_map/ppermute | solution.py:756
  15.0 1.3 %copy-start.2 = (s32[2,29]{1,0:T(2,128)S(1)}, s32[2,29]{1,0:T(2,128)}, u32[]{:S(2)}) copy-start(s32[2,29]{1,0:T(2,128)} %constant.12.clone.tab) | copy-start | bytes 700
  15.0 26.0 %collective-permute-start.1 = (f32[576,128]{1,0:T(8,128)}, f32[576,128]{1,0:T(8,128)S(1)}, u32[]{:S(2)}, u32[]{:S(2)}) collective-permute-start(f32[576,128]{1,0:T(8,128)} %get-tuple-element.25), channel_id=1, source_target_pairs={{1,0},{2,1},{3,2},{4,3},{5,4},{6,5},{7,6},{8,7},{9,8},{10,9},{11,1... | collective-permute-start | bytes 884744 | tf_op jit(solution)/shard_map/ppermute | solution.py:756
  16.3 1.2 %copy-start = (f32[1728,128]{1,0:T(8,128)S(1)}, f32[1728,128]{1,0:T(8,128)}, u32[]{:S(2)}) copy-start(f32[1728,128]{1,0:T(8,128)} %get-tuple-element.23.own) | copy-start | bytes 2654212
  41.2 13.7 %collective-permute-start.4 = (f32[640,128]{1,0:T(8,128)S(1)}, f32[640,128]{1,0:T(8,128)S(1)}, u32[]{:S(2)}, u32[]{:S(2)}) collective-permute-start(f32[640,128]{1,0:T(8,128)S(1)} %get-tuple-element.36), channel_id=1, source_target_pairs={{0,1},{1,2},{2,3},{3,4},{4,5},{5,6},{6,7},{7,8},{8,9},{9,10},{10,1... | collective-permute-start | bytes 983048 | tf_op jit(solution)/shard_map/ppermute | solution.py:756
  47.0 1.3 %copy-start.1 = (s32[2,34]{1,0:T(2,128)S(1)}, s32[2,34]{1,0:T(2,128)}, u32[]{:S(2)}) copy-start(s32[2,34]{1,0:T(2,128)} %constant.13.clone.tab) | copy-start | bytes 820
  47.0 20.1 %collective-permute-start.5 = (f32[640,128]{1,0:T(8,128)S(1)}, f32[640,128]{1,0:T(8,128)S(1)}, u32[]{:S(2)}, u32[]{:S(2)}) collective-permute-start(f32[640,128]{1,0:T(8,128)S(1)} %get-tuple-element.37), channel_id=1, source_target_pairs={{1,0},{2,1},{3,2},{4,3},{5,4},{6,5},{7,6},{8,7},{9,8},{10,9},{11,1... | collective-permute-start | bytes 983048 | tf_op jit(solution)/shard_map/ppermute | solution.py:756
where the time goes:
time: 114 us
  Pallas kernels  45.3 us (40%)
  blocking collectives  31.8 us (28%)
  starting transfers between devices  20.2 us (18%)
  waiting for transfers between devices  12.2 us (11%)
  between operations  1.56 us (1%)
  other arithmetic  1.37 us (1%)
  local copies, waits for them, and re-layouts  1.25 us (1%)
    pallas_call x5, Pallas kernels, call(): pl.pallas_call(body, out_shape=outs, in_specs=specs, out_specs=jax.tree.m...  45.3 us
    all_to_all x1, blocking collectives, on_device(): lax.all_to_all(jnp.broadcast_to(top[:1][None], (devices, 1, 128)), GX + Y...  31.8 us
    ppermute x3, starting transfers between devices, exchange(): lax.ppermute(onward, axis, ring(axis, 1))  15.7 us
    ppermute x3, waiting for transfers between devices, exchange(): lax.ppermute(backward, axis, ring(axis, -1))  12.2 us
    ppermute x3, starting transfers between devices, exchange(): lax.ppermute(backward, axis, ring(axis, -1))  4.5 us
  transfers between devices with their start and end apart: 6, of which 1 were waited for; matrix products, arithmetic and copies ran while one was open for 0% of the time, Pallas kernels for 26%

commit v1 on v0

--- a/solution.py
+++ b/solution.py
@@ -53,14 +53,14 @@
 
 def slope(dx, dy, dz):
     squared = dx * dx + dy * dy + dz * dz
-    distance = squared * lax.rsqrt(jnp.maximum(squared, 1e-30))
+    distance = pl.reciprocal(lax.rsqrt(squared), approx=True)
     remain = jnp.maximum(1.0 - distance, 0.0)
     return squared, remain * remain * remain
 
 
 def weight(dx, dy, dz):
     squared = dx * dx + dy * dy + dz * dz
-    distance = squared * lax.rsqrt(jnp.maximum(squared, 1e-30))
+    distance = pl.reciprocal(lax.rsqrt(squared), approx=True)
     remain = jnp.maximum(1.0 - distance, 0.0)
     twice = remain * remain
     return (twice * twice) * (4.0 * distance + 1.0)
@@ -371,23 +371,26 @@
         q, n = tab[0, e], tab[1, e]
         sources = [(near, n * ROWS, PART)]
         sources += [(rolled, (v * len(SIDES) + n) * 128, DENSE) for v in range(2)]
+        for h in range(2):
+            against(own, q, h, sources, total)
+        return carry
+
+    def sparse_pair(e, carry):
+        q, n = tab[0, e], tab[1, e]
+        sources = [(near, n * ROWS, PART)]
+        sources += [(rolled, (v * len(SIDES) + n) * 128, DENSE) for v in range(2)]
         against(own, q, 0, sources, total, 0, 8)
-
-        @pl.when(many_near)
-        def _():
-            against(own, q, 0, sources, total, 8, 16)
-
-        @pl.when(many_own)
-        def _():
-            against(own, q, 1, sources, total, 0, 8)
-
-        @pl.when(many_own & many_near)
-        def _():
-            against(own, q, 1, sources, total, 8, 16)
-
         return carry
 
-    lax.fori_loop(0, count, pair, 0)
+    few = jnp.logical_not(many_own | many_near)
+
+    @pl.when(few)
+    def _():
+        lax.fori_loop(0, count, sparse_pair, 0)
+
+    @pl.when(jnp.logical_not(few))
+    def _():
+        lax.fori_loop(0, count, pair, 0)
 
 
 def sum_walls(spots, sources):
@@ -698,6 +701,13 @@
     top[...] = jnp.zeros(top.shape, F32) + jnp.max(most)
 
 
+def scale_body(tops, acc, out):
+    largest = jnp.broadcast_to(jnp.max(tops[...], axis=0), (8, 128))
+    step = 0.25 * jnp.sqrt(0.5 / (jnp.sqrt(largest) + 1e-6))
+    for n in range(3 * SLOTS * COLS // 8):
+        out[8 * n : 8 * n + 8, :] = acc[8 * n : 8 * n + 8, :] * step
+
+
 def shape(*dims):
     return jax.ShapeDtypeStruct(dims, F32)
 
@@ -789,9 +799,8 @@
     )
     devices = lax.axis_size(GX + YZ)
     tops = lax.all_to_all(jnp.broadcast_to(top[:1][None], (devices, 1, 128)), GX + YZ, 0, 0, tiled=True)
-    largest = jnp.max(tops)
-    step = 0.25 * jnp.sqrt(0.5 / (jnp.sqrt(largest) + 1e-6))
-    return step * acc.reshape(fluid_offsets.shape), rate.reshape(fluid_density.shape)
+    out = call(scale_body, shape(3 * SLOTS * COLS, 128), (tops, acc), name="scale")
+    return out.reshape(fluid_offsets.shape), rate.reshape(fluid_density.shape)
 
 
 def solution(mesh):

time: 114 us -> 112 us (0.982)
  other arithmetic: 1.37 us -> 0 us
    pallas_call x5 -> x6, Pallas kernels: 45.3 us -> 44.5 us  [call(): pl.pallas_call(body, out_shape=outs, in_specs=specs, out_specs=jax.tree.m...]
where the time goes in v1:
time: 112 us
  Pallas kernels  44.5 us (40%)
  blocking collectives  31.8 us (28%)
  starting transfers between devices  20.2 us (18%)
  waiting for transfers between devices  13 us (12%)
  local copies, waits for them, and re-layouts  1.25 us (1%)
    pallas_call x6, Pallas kernels, call(): pl.pallas_call(body, out_shape=outs, in_specs=specs, out_specs=jax.tree.m...  44.5 us
    all_to_all x1, blocking collectives, on_device(): lax.all_to_all(jnp.broadcast_to(top[:1][None], (devices, 1, 128)), GX + Y...  31.8 us
    ppermute x3, starting transfers between devices, exchange(): lax.ppermute(onward, axis, ring(axis, 1))  15.7 us
    ppermute x3, waiting for transfers between devices, exchange(): lax.ppermute(backward, axis, ring(axis, -1))  12.9 us
    ppermute x3, starting transfers between devices, exchange(): lax.ppermute(backward, axis, ring(axis, -1))  4.5 us
  transfers between devices with their start and end apart: 6, of which 1 were waited for; matrix products, arithmetic and copies ran while one was open for 0% of the time, Pallas kernels for 26%

profile of v1, /device:TPU:1, one launch (start us, length us, event | category | flops | bytes accessed | tf_op | source)
XLA Modules:
  0.0 111.5 jit_solution(9621977562106827169)
XLA Ops:
  0.6 2.6 %pack.1 = (f32[1728,128]{1,0:T(8,128)}, f32[768,128]{1,0:T(8,128)}, f32[768,128]{1,0:T(8,128)}, f32[576,128]{1,0:T(8,128)}, f32[576,128]{1,0:T(8,128)}) custom-call(f32[576,128]{1,0:T(8,128)} %bitcast.8, f32[576,128]{1,0:T(8,128)} %bitcast.9, f32[192,128]{1,0:T(8,128)} %bitcast.11, s32[3,4,128]{2,1,0:T(4,128)} %cnt_in.1, f32[144,128]{1,0:T(8,128)} %bitcast.12, ...), custom_call_target="tpu_custom_call" | custom-call | bytes 1000000 | tf_op jit(solution)/shard_map/pack/pallas_call | solution.py:722
  3.2 4.9 %collective-permute-start.2 = (f32[768,128]{1,0:T(8,128)}, f32[768,128]{1,0:T(8,128)S(1)}, u32[]{:S(2)}, u32[]{:S(2)}) collective-permute-start(f32[768,128]{1,0:T(8,128)} %get-tuple-element.26), channel_id=1, source_target_pairs={{0,16},{16,32},{32,48},{48,64},{64,80},{80,96},{96,112},{112,128},... | collective-permute-start | bytes 1179656 | tf_op jit(solution)/shard_map/ppermute | solution.py:766
  8.2 1.9 %collective-permute-start.3 = (f32[768,128]{1,0:T(8,128)}, f32[768,128]{1,0:T(8,128)S(1)}, u32[]{:S(2)}, u32[]{:S(2)}) collective-permute-start(f32[768,128]{1,0:T(8,128)} %get-tuple-element.27), channel_id=1, source_target_pairs={{16,0},{32,16},{48,32},{64,48},{80,64},{96,80},{112,96},{128,112},... | collective-permute-start | bytes 1179656 | tf_op jit(solution)/shard_map/ppermute | solution.py:766
  10.1 4.9 %collective-permute-start = (f32[576,128]{1,0:T(8,128)}, f32[576,128]{1,0:T(8,128)S(1)}, u32[]{:S(2)}, u32[]{:S(2)}) collective-permute-start(f32[576,128]{1,0:T(8,128)} %get-tuple-element.24), channel_id=1, source_target_pairs={{0,1},{1,2},{2,3},{3,4},{4,5},{5,6},{6,7},{7,8},{8,9},{9,10},{10,1... | collective-permute-start | bytes 884744 | tf_op jit(solution)/shard_map/ppermute | solution.py:766
  15.0 0.0 copy-start.2
  15.0 1.3 %collective-permute-start.1 = (f32[576,128]{1,0:T(8,128)}, f32[576,128]{1,0:T(8,128)S(1)}, u32[]{:S(2)}, u32[]{:S(2)}) collective-permute-start(f32[576,128]{1,0:T(8,128)} %get-tuple-element.25), channel_id=1, source_target_pairs={{1,0},{2,1},{3,2},{4,3},{5,4},{6,5},{7,6},{8,7},{9,8},{10,9},{11,1... | collective-permute-start | bytes 884744 | tf_op jit(solution)/shard_map/ppermute | solution.py:766
  16.3 0.0 copy-done.2
  16.3 0.0 copy-start
  16.3 1.2 %copy-done = f32[1728,128]{1,0:T(8,128)S(1)} copy-done((f32[1728,128]{1,0:T(8,128)S(1)}, f32[1728,128]{1,0:T(8,128)}, u32[]{:S(2)}) %copy-start) | copy-done | bytes 884760
  17.5 23.2 %inner.1 = f32[768,128]{1,0:T(8,128)S(1)} custom-call(s32[2,29]{1,0:T(2,128)S(1)} %copy-done.2, f32[1728,128]{1,0:T(8,128)S(1)} %copy-done), custom_call_target="tpu_custom_call" | custom-call | flops 60000000 | bytes 1000000 | tf_op jit(solution)/shard_map/inner/pallas_call | solution.py:722
  40.7 0.0 collective-permute-done.from_down.down_side
  40.7 0.0 collective-permute-done.1.from_up.up_side
  40.7 0.0 collective-permute-done.2.from_left
  40.7 0.0 collective-permute-done.3.from_right
  40.7 0.1 forward.1
  40.8 5.8 %collective-permute-start.4 = (f32[640,128]{1,0:T(8,128)S(1)}, f32[640,128]{1,0:T(8,128)S(1)}, u32[]{:S(2)}, u32[]{:S(2)}) collective-permute-start(f32[640,128]{1,0:T(8,128)S(1)} %get-tuple-element.36), channel_id=1, source_target_pairs={{0,1},{1,2},{2,3},{3,4},{4,5},{5,6},{6,7},{7,8},{8,9},{9,10},{10,1... | collective-permute-start | bytes 983048 | tf_op jit(solution)/shard_map/ppermute | solution.py:766
  46.7 0.0 copy-start.1
  46.7 1.3 %collective-permute-start.5 = (f32[640,128]{1,0:T(8,128)S(1)}, f32[640,128]{1,0:T(8,128)S(1)}, u32[]{:S(2)}, u32[]{:S(2)}) collective-permute-start(f32[640,128]{1,0:T(8,128)S(1)} %get-tuple-element.37), channel_id=1, source_target_pairs={{1,0},{2,1},{3,2},{4,3},{5,4},{6,5},{7,6},{8,7},{9,8},{10,9},{11,1... | collective-permute-start | bytes 983048 | tf_op jit(solution)/shard_map/ppermute | solution.py:766
  48.0 0.0 copy-done.1
  48.0 5.8 %sides.1 = (f32[2016,128]{1,0:T(8,128)S(1)}, f32[768,128]{1,0:T(8,128)S(1)}) custom-call(s32[2,34]{1,0:T(2,128)S(1)} %copy-done.1, f32[1728,128]{1,0:T(8,128)S(1)} %copy-done, f32[1664,128]{1,0:T(8,128)S(1)} %get-tuple-element.30.halo, f32[576,128]{1,0:T(8,128)S(1)} %collective-permute-done.from_down.down_side, ...), custom_call_target="tpu_custom_call" | custom-call | flops 60000000 | bytes 1000000 | tf_op jit(solution)/shard_map/sides/pallas_call | solution.py:722
  53.8 0.0 collective-permute-done.4.down_corner
  53.8 12.9 %collective-permute-done.5.up_corner = f32[640,128]{1,0:T(8,128)S(1)} collective-permute-done((f32[640,128]{1,0:T(8,128)S(1)}, f32[640,128]{1,0:T(8,128)S(1)}, u32[]{:S(2)}, u32[]{:S(2)}) %collective-permute-start.5) | collective-permute-done | bytes 327712 | tf_op jit(solution)/shard_map/ppermute | solution.py:766
  66.8 12.0 %rim.1 = (f32[576,128]{1,0:T(8,128)S(1)}, f32[192,128]{1,0:T(8,128)}, f32[8,128]{1,0:T(8,128)S(1)}) custom-call(f32[1728,128]{1,0:T(8,128)S(1)} %copy-done, f32[1664,128]{1,0:T(8,128)S(1)} %get-tuple-element.30.halo, f32[2016,128]{1,0:T(8,128)S(1)} %get-tuple-element.34.near, f32[576,128]{1,0:T(8,128)S(1)} %collective-permute-done.from_down.down_side, ...), custom_call_target="tpu_custom_call" | custom-call | bytes 1000000 | tf_op jit(solution)/shard_map/rim/pallas_call | solution.py:722
  78.8 0.1 broadcast_in_dim.9
  78.8 31.8 %all_to_all.5.tops = f32[256,1,128]{2,1,0:T(1,128)S(1)} all-to-all(f32[256,1,128]{2,1,0:T(1,128)S(1)} %broadcast_in_dim.9), channel_id=1, replica_groups=mesh['gx_0'=4,'gx_1'=2,'gx_2'=2,'yz_0'=4,'yz_1'=4] {'gx_0','gx_1','gx_2'..., dimensions={0} | all-to-all | bytes 262144 | tf_op jit(solution)/shard_map/all_to_all | solution.py:801
  110.7 0.8 scale.1
  (1 shorter events, 0.0 us)
Async XLA Ops:
  3.2 37.5 %collective-permute-start.2 = (f32[768,128]{1,0:T(8,128)}, f32[768,128]{1,0:T(8,128)S(1)}, u32[]{:S(2)}, u32[]{:S(2)}) collective-permute-start(f32[768,128]{1,0:T(8,128)} %get-tuple-element.26), channel_id=1, source_target_pairs={{0,16},{16,32},{32,48},{48,64},{64,80},{80,96},{96,112},{112,128},... | collective-permute-start | bytes 1179656 | tf_op jit(solution)/shard_map/ppermute | solution.py:766
  8.2 32.6 %collective-permute-start.3 = (f32[768,128]{1,0:T(8,128)}, f32[768,128]{1,0:T(8,128)S(1)}, u32[]{:S(2)}, u32[]{:S(2)}) collective-permute-start(f32[768,128]{1,0:T(8,128)} %get-tuple-element.27), channel_id=1, source_target_pairs={{16,0},{32,16},{48,32},{64,48},{80,64},{96,80},{112,96},{128,112},... | collective-permute-start | bytes 1179656 | tf_op jit(solution)/shard_map/ppermute | solution.py:766
  10.1 30.6 %collective-permute-start = (f32[576,128]{1,0:T(8,128)}, f32[576,128]{1,0:T(8,128)S(1)}, u32[]{:S(2)}, u32[]{:S(2)}) collective-permute-start(f32[576,128]{1,0:T(8,128)} %get-tuple-element.24), channel_id=1, source_target_pairs={{0,1},{1,2},{2,3},{3,4},{4,5},{5,6},{6,7},{7,8},{8,9},{9,10},{10,1... | collective-permute-start | bytes 884744 | tf_op jit(solution)/shard_map/ppermute | solution.py:766
  15.0 1.3 %copy-start.2 = (s32[2,29]{1,0:T(2,128)S(1)}, s32[2,29]{1,0:T(2,128)}, u32[]{:S(2)}) copy-start(s32[2,29]{1,0:T(2,128)} %constant.4.clone.tab) | copy-start | bytes 700
  15.0 25.7 %collective-permute-start.1 = (f32[576,128]{1,0:T(8,128)}, f32[576,128]{1,0:T(8,128)S(1)}, u32[]{:S(2)}, u32[]{:S(2)}) collective-permute-start(f32[576,128]{1,0:T(8,128)} %get-tuple-element.25), channel_id=1, source_target_pairs={{1,0},{2,1},{3,2},{4,3},{5,4},{6,5},{7,6},{8,7},{9,8},{10,9},{11,1... | collective-permute-start | bytes 884744 | tf_op jit(solution)/shard_map/ppermute | solution.py:766
  16.3 1.2 %copy-start = (f32[1728,128]{1,0:T(8,128)S(1)}, f32[1728,128]{1,0:T(8,128)}, u32[]{:S(2)}) copy-start(f32[1728,128]{1,0:T(8,128)} %get-tuple-element.23.own) | copy-start | bytes 2654212
  40.8 13.0 %collective-permute-start.4 = (f32[640,128]{1,0:T(8,128)S(1)}, f32[640,128]{1,0:T(8,128)S(1)}, u32[]{:S(2)}, u32[]{:S(2)}) collective-permute-start(f32[640,128]{1,0:T(8,128)S(1)} %get-tuple-element.36), channel_id=1, source_target_pairs={{0,1},{1,2},{2,3},{3,4},{4,5},{5,6},{6,7},{7,8},{8,9},{9,10},{10,1... | collective-permute-start | bytes 983048 | tf_op jit(solution)/shard_map/ppermute | solution.py:766
  46.7 1.3 %copy-start.1 = (s32[2,34]{1,0:T(2,128)S(1)}, s32[2,34]{1,0:T(2,128)}, u32[]{:S(2)}) copy-start(s32[2,34]{1,0:T(2,128)} %constant.5.clone.tab) | copy-start | bytes 820
  46.7 20.1 %collective-permute-start.5 = (f32[640,128]{1,0:T(8,128)S(1)}, f32[640,128]{1,0:T(8,128)S(1)}, u32[]{:S(2)}, u32[]{:S(2)}) collective-permute-start(f32[640,128]{1,0:T(8,128)S(1)} %get-tuple-element.37), channel_id=1, source_target_pairs={{1,0},{2,1},{3,2},{4,3},{5,4},{6,5},{7,6},{8,7},{9,8},{10,9},{11,1... | collective-permute-start | bytes 983048 | tf_op jit(solution)/shard_map/ppermute | solution.py:766

commit v2 on v1

--- a/solution.py
+++ b/solution.py
@@ -247,26 +247,28 @@
     roll_columns(own, rolled, COLS)
 
     def block(t, s, v, symmetric):
-        for h in range(2):
-            if v == 0:
-                src = [rows8(own, s * ROWS + PART[k] + 8 * h) for k in range(8)]
-            else:
-                src = [rows8(rolled, ((v - 1) * COLS + s) * 128 + 16 * k + 8 * h) for k in range(8)]
-            back = [zero] * 4
-            for i in range(SLOTS):
-                dst = [spread(own, t * ROWS + PART[k] + i) for k in range(8)]
-                terms = fluid_pair(dst, src)
-                for c in range(4):
-                    base = ((t * 4 + c) * SLOTS + i) * 8
-                    put8(acc, base, rows8(acc, base) + terms[c])
-                if symmetric:
+        if v == 0:
+            src = [[rows8(own, s * ROWS + PART[k] + 8 * h) for k in range(8)] for h in range(2)]
+        else:
+            base = ((v - 1) * COLS + s) * 128
+            src = [[rows8(rolled, base + 16 * k + 8 * h) for k in range(8)] for h in range(2)]
+        back = [[zero] * 4 for _ in range(2)]
+        for i in range(SLOTS):
+            dst = [spread(own, t * ROWS + PART[k] + i) for k in range(8)]
+            both = [fluid_pair(dst, src[h]) for h in range(2)]
+            for c in range(4):
+                base = ((t * 4 + c) * SLOTS + i) * 8
+                put8(acc, base, rows8(acc, base) + (both[0][c] + both[1][c]))
+            if symmetric:
+                for h in range(2):
                     for c in range(3):
-                        back[c] = back[c] - terms[c]
-                    back[3] = back[3] + terms[3]
-            if symmetric:
+                        back[h][c] = back[h][c] - both[h][c]
+                    back[h][3] = back[h][3] + both[h][3]
+        if symmetric:
+            for h in range(2):
                 for c in range(4):
                     base = (s * 3 + v) * 64 + 16 * c + 8 * h
-                    put8(racc, base, rows8(racc, base) + back[c])
+                    put8(racc, base, rows8(racc, base) + back[h][c])
 
     def pair(e, c):
         t, s = tab[0, e], tab[1, e]
@@ -332,16 +334,18 @@
     return pltpu.roll(value, shift % 128, 1) if shift % 128 else value
 
 
-def against(own, q, h, sources, total, first=0, last=SLOTS):
-    t = [rows8(own, q * ROWS + PART[k] + 8 * h) for k in range(8)]
-    sums = [jnp.zeros((8, 128), F32)] * 4
+def against(own, q, sources, total, halves=2, slots=SLOTS):
+    t = [[rows8(own, q * ROWS + PART[k] + 8 * h) for k in range(8)] for h in range(halves)]
+    sums = [[jnp.zeros((8, 128), F32)] * 4 for _ in range(halves)]
     for ref, base, at in sources:
-        for j in range(first, last):
-            terms = fluid_pair(t, [spread(ref, base + at[k] + j) for k in range(8)])
-            sums = [a + b for a, b in zip(sums, terms)]
-    for c in range(4):
-        base = q * 64 + 16 * c + 8 * h
-        put8(total, base, rows8(total, base) + sums[c])
+        for j in range(slots):
+            s = [spread(ref, base + at[k] + j) for k in range(8)]
+            for h in range(halves):
+                sums[h] = [a + b for a, b in zip(sums[h], fluid_pair(t[h], s))]
+    for h in range(halves):
+        for c in range(4):
+            base = q * 64 + 16 * c + 8 * h
+            put8(total, base, rows8(total, base) + sums[h][c])
 
 
 DENSE = tuple(16 * k for k in range(8))
@@ -371,15 +375,14 @@
         q, n = tab[0, e], tab[1, e]
         sources = [(near, n * ROWS, PART)]
         sources += [(rolled, (v * len(SIDES) + n) * 128, DENSE) for v in range(2)]
-        for h in range(2):
-            against(own, q, h, sources, total)
+        against(own, q, sources, total)
         return carry
 
     def sparse_pair(e, carry):
         q, n = tab[0, e], tab[1, e]
         sources = [(near, n * ROWS, PART)]
         sources += [(rolled, (v * len(SIDES) + n) * 128, DENSE) for v in range(2)]
-        against(own, q, 0, sources, total, 0, 8)
+        against(own, q, sources, total, 1, 8)
         return carry
 
     few = jnp.logical_not(many_own | many_near)
@@ -426,8 +429,7 @@
         q = min(max(fx, 0), BX - 1) * BY + min(max(fy, 0), BY - 1)
         sources = [(corner, n * ROWS, PART)]
         sources += [(rolled, (v * len(CORNERS) + n) * 128, DENSE) for v in range(2)]
-        for h in range(2):
-            against(own, q, h, sources, total)
+        against(own, q, sources, total)
 
     def place(fx, fy):
         if 0 <= fx < BX and 0 <= fy < BY:

time: 112 us -> 112 us (level); the launches traced: 112 us -> 113 us
  blocking collectives: 31.8 us -> 33.2 us
    all_to_all x1, blocking collectives: 31.8 us -> 33.2 us  [on_device(): lax.all_to_all(jnp.broadcast_to(top[:1][None], (devices, 1, 128)), GX + Y...]
where the time goes in v2:
time: 112 us; the launch traced here: 113 us
  Pallas kernels  44.7 us (40%)
  blocking collectives  33.2 us (30%)
  starting transfers between devices  20.2 us (18%)
  waiting for transfers between devices  13 us (12%)
  local copies, waits for them, and re-layouts  1.25 us (1%)
    pallas_call x6, Pallas kernels, call(): pl.pallas_call(body, out_shape=outs, in_specs=specs, out_specs=jax.tree.m...  44.7 us
    all_to_all x1, blocking collectives, on_device(): lax.all_to_all(jnp.broadcast_to(top[:1][None], (devices, 1, 128)), GX + Y...  33.2 us
    ppermute x3, starting transfers between devices, exchange(): lax.ppermute(onward, axis, ring(axis, 1))  15.7 us
    ppermute x3, waiting for transfers between devices, exchange(): lax.ppermute(backward, axis, ring(axis, -1))  12.9 us
    ppermute x3, starting transfers between devices, exchange(): lax.ppermute(backward, axis, ring(axis, -1))  4.5 us
  transfers between devices with their start and end apart: 6, of which 1 were waited for; matrix products, arithmetic and copies ran while one was open for 0% of the time, Pallas kernels for 26%

profile of v2, /device:TPU:1, one launch (start us, length us, event | category | flops | bytes accessed | tf_op | source)
XLA Modules:
  0.0 113.0 jit_solution(15659310083445467523)
XLA Ops:
  0.6 2.6 %pack.1 = (f32[1728,128]{1,0:T(8,128)}, f32[768,128]{1,0:T(8,128)}, f32[768,128]{1,0:T(8,128)}, f32[576,128]{1,0:T(8,128)}, f32[576,128]{1,0:T(8,128)}) custom-call(f32[576,128]{1,0:T(8,128)} %bitcast.8, f32[576,128]{1,0:T(8,128)} %bitcast.9, f32[192,128]{1,0:T(8,128)} %bitcast.11, s32[3,4,128]{2,1,0:T(4,128)} %cnt_in.1, f32[144,128]{1,0:T(8,128)} %bitcast.12, ...), custom_call_target="tpu_custom_call" | custom-call | bytes 1000000 | tf_op jit(solution)/shard_map/pack/pallas_call | solution.py:724
  3.2 4.9 %collective-permute-start.2 = (f32[768,128]{1,0:T(8,128)}, f32[768,128]{1,0:T(8,128)S(1)}, u32[]{:S(2)}, u32[]{:S(2)}) collective-permute-start(f32[768,128]{1,0:T(8,128)} %get-tuple-element.26), channel_id=1, source_target_pairs={{0,16},{16,32},{32,48},{48,64},{64,80},{80,96},{96,112},{112,128},... | collective-permute-start | bytes 1179656 | tf_op jit(solution)/shard_map/ppermute | solution.py:768
  8.2 1.9 %collective-permute-start.3 = (f32[768,128]{1,0:T(8,128)}, f32[768,128]{1,0:T(8,128)S(1)}, u32[]{:S(2)}, u32[]{:S(2)}) collective-permute-start(f32[768,128]{1,0:T(8,128)} %get-tuple-element.27), channel_id=1, source_target_pairs={{16,0},{32,16},{48,32},{64,48},{80,64},{96,80},{112,96},{128,112},... | collective-permute-start | bytes 1179656 | tf_op jit(solution)/shard_map/ppermute | solution.py:768
  10.1 4.9 %collective-permute-start = (f32[576,128]{1,0:T(8,128)}, f32[576,128]{1,0:T(8,128)S(1)}, u32[]{:S(2)}, u32[]{:S(2)}) collective-permute-start(f32[576,128]{1,0:T(8,128)} %get-tuple-element.24), channel_id=1, source_target_pairs={{0,1},{1,2},{2,3},{3,4},{4,5},{5,6},{6,7},{7,8},{8,9},{9,10},{10,1... | collective-permute-start | bytes 884744 | tf_op jit(solution)/shard_map/ppermute | solution.py:768
  15.0 0.0 copy-start.2
  15.0 1.3 %collective-permute-start.1 = (f32[576,128]{1,0:T(8,128)}, f32[576,128]{1,0:T(8,128)S(1)}, u32[]{:S(2)}, u32[]{:S(2)}) collective-permute-start(f32[576,128]{1,0:T(8,128)} %get-tuple-element.25), channel_id=1, source_target_pairs={{1,0},{2,1},{3,2},{4,3},{5,4},{6,5},{7,6},{8,7},{9,8},{10,9},{11,1... | collective-permute-start | bytes 884744 | tf_op jit(solution)/shard_map/ppermute | solution.py:768
  16.3 0.0 copy-done.2
  16.3 0.0 copy-start
  16.3 1.2 %copy-done = f32[1728,128]{1,0:T(8,128)S(1)} copy-done((f32[1728,128]{1,0:T(8,128)S(1)}, f32[1728,128]{1,0:T(8,128)}, u32[]{:S(2)}) %copy-start) | copy-done | bytes 884760
  17.5 23.2 %inner.1 = f32[768,128]{1,0:T(8,128)S(1)} custom-call(s32[2,29]{1,0:T(2,128)S(1)} %copy-done.2, f32[1728,128]{1,0:T(8,128)S(1)} %copy-done), custom_call_target="tpu_custom_call" | custom-call | flops 60000000 | bytes 1000000 | tf_op jit(solution)/shard_map/inner/pallas_call | solution.py:724
  40.7 0.0 collective-permute-done.from_down.down_side
  40.7 0.0 collective-permute-done.1.from_up.up_side
  40.7 0.0 collective-permute-done.2.from_left
  40.8 0.0 collective-permute-done.3.from_right
  40.8 0.1 forward.1
  40.9 5.8 %collective-permute-start.4 = (f32[640,128]{1,0:T(8,128)S(1)}, f32[640,128]{1,0:T(8,128)S(1)}, u32[]{:S(2)}, u32[]{:S(2)}) collective-permute-start(f32[640,128]{1,0:T(8,128)S(1)} %get-tuple-element.36), channel_id=1, source_target_pairs={{0,1},{1,2},{2,3},{3,4},{4,5},{5,6},{6,7},{7,8},{8,9},{9,10},{10,1... | collective-permute-start | bytes 983048 | tf_op jit(solution)/shard_map/ppermute | solution.py:768
  46.7 0.0 copy-start.1
  46.7 1.3 %collective-permute-start.5 = (f32[640,128]{1,0:T(8,128)S(1)}, f32[640,128]{1,0:T(8,128)S(1)}, u32[]{:S(2)}, u32[]{:S(2)}) collective-permute-start(f32[640,128]{1,0:T(8,128)S(1)} %get-tuple-element.37), channel_id=1, source_target_pairs={{1,0},{2,1},{3,2},{4,3},{5,4},{6,5},{7,6},{8,7},{9,8},{10,9},{11,1... | collective-permute-start | bytes 983048 | tf_op jit(solution)/shard_map/ppermute | solution.py:768
  48.0 0.0 copy-done.1
  48.0 5.8 %sides.1 = (f32[2016,128]{1,0:T(8,128)S(1)}, f32[768,128]{1,0:T(8,128)S(1)}) custom-call(s32[2,34]{1,0:T(2,128)S(1)} %copy-done.1, f32[1728,128]{1,0:T(8,128)S(1)} %copy-done, f32[1664,128]{1,0:T(8,128)S(1)} %get-tuple-element.30.halo, f32[576,128]{1,0:T(8,128)S(1)} %collective-permute-done.from_down.down_side, ...), custom_call_target="tpu_custom_call" | custom-call | flops 60000000 | bytes 1000000 | tf_op jit(solution)/shard_map/sides/pallas_call | solution.py:724
  53.9 0.0 collective-permute-done.4.down_corner
  53.9 12.9 %collective-permute-done.5.up_corner = f32[640,128]{1,0:T(8,128)S(1)} collective-permute-done((f32[640,128]{1,0:T(8,128)S(1)}, f32[640,128]{1,0:T(8,128)S(1)}, u32[]{:S(2)}, u32[]{:S(2)}) %collective-permute-start.5) | collective-permute-done | bytes 327712 | tf_op jit(solution)/shard_map/ppermute | solution.py:768
  66.8 12.2 %rim.1 = (f32[576,128]{1,0:T(8,128)S(1)}, f32[192,128]{1,0:T(8,128)}, f32[8,128]{1,0:T(8,128)S(1)}) custom-call(f32[1728,128]{1,0:T(8,128)S(1)} %copy-done, f32[1664,128]{1,0:T(8,128)S(1)} %get-tuple-element.30.halo, f32[2016,128]{1,0:T(8,128)S(1)} %get-tuple-element.34.near, f32[576,128]{1,0:T(8,128)S(1)} %collective-permute-done.from_down.down_side, ...), custom_call_target="tpu_custom_call" | custom-call | bytes 1000000 | tf_op jit(solution)/shard_map/rim/pallas_call | solution.py:724
  79.0 0.1 broadcast_in_dim.9
  79.0 33.2 %all_to_all.5.tops = f32[256,1,128]{2,1,0:T(1,128)S(1)} all-to-all(f32[256,1,128]{2,1,0:T(1,128)S(1)} %broadcast_in_dim.9), channel_id=1, replica_groups=mesh['gx_0'=4,'gx_1'=2,'gx_2'=2,'yz_0'=4,'yz_1'=4] {'gx_0','gx_1','gx_2'..., dimensions={0} | all-to-all | bytes 262144 | tf_op jit(solution)/shard_map/all_to_all | solution.py:803
  112.2 0.8 scale.1
  (1 shorter events, 0.0 us)
Async XLA Ops:
  3.2 37.5 %collective-permute-start.2 = (f32[768,128]{1,0:T(8,128)}, f32[768,128]{1,0:T(8,128)S(1)}, u32[]{:S(2)}, u32[]{:S(2)}) collective-permute-start(f32[768,128]{1,0:T(8,128)} %get-tuple-element.26), channel_id=1, source_target_pairs={{0,16},{16,32},{32,48},{48,64},{64,80},{80,96},{96,112},{112,128},... | collective-permute-start | bytes 1179656 | tf_op jit(solution)/shard_map/ppermute | solution.py:768
  8.2 32.6 %collective-permute-start.3 = (f32[768,128]{1,0:T(8,128)}, f32[768,128]{1,0:T(8,128)S(1)}, u32[]{:S(2)}, u32[]{:S(2)}) collective-permute-start(f32[768,128]{1,0:T(8,128)} %get-tuple-element.27), channel_id=1, source_target_pairs={{16,0},{32,16},{48,32},{64,48},{80,64},{96,80},{112,96},{128,112},... | collective-permute-start | bytes 1179656 | tf_op jit(solution)/shard_map/ppermute | solution.py:768
  10.1 30.6 %collective-permute-start = (f32[576,128]{1,0:T(8,128)}, f32[576,128]{1,0:T(8,128)S(1)}, u32[]{:S(2)}, u32[]{:S(2)}) collective-permute-start(f32[576,128]{1,0:T(8,128)} %get-tuple-element.24), channel_id=1, source_target_pairs={{0,1},{1,2},{2,3},{3,4},{4,5},{5,6},{6,7},{7,8},{8,9},{9,10},{10,1... | collective-permute-start | bytes 884744 | tf_op jit(solution)/shard_map/ppermute | solution.py:768
  15.0 1.3 %copy-start.2 = (s32[2,29]{1,0:T(2,128)S(1)}, s32[2,29]{1,0:T(2,128)}, u32[]{:S(2)}) copy-start(s32[2,29]{1,0:T(2,128)} %constant.4.clone.tab) | copy-start | bytes 700
  15.0 25.7 %collective-permute-start.1 = (f32[576,128]{1,0:T(8,128)}, f32[576,128]{1,0:T(8,128)S(1)}, u32[]{:S(2)}, u32[]{:S(2)}) collective-permute-start(f32[576,128]{1,0:T(8,128)} %get-tuple-element.25), channel_id=1, source_target_pairs={{1,0},{2,1},{3,2},{4,3},{5,4},{6,5},{7,6},{8,7},{9,8},{10,9},{11,1... | collective-permute-start | bytes 884744 | tf_op jit(solution)/shard_map/ppermute | solution.py:768
  16.3 1.2 %copy-start = (f32[1728,128]{1,0:T(8,128)S(1)}, f32[1728,128]{1,0:T(8,128)}, u32[]{:S(2)}) copy-start(f32[1728,128]{1,0:T(8,128)} %get-tuple-element.23.own) | copy-start | bytes 2654212
  40.9 13.0 %collective-permute-start.4 = (f32[640,128]{1,0:T(8,128)S(1)}, f32[640,128]{1,0:T(8,128)S(1)}, u32[]{:S(2)}, u32[]{:S(2)}) collective-permute-start(f32[640,128]{1,0:T(8,128)S(1)} %get-tuple-element.36), channel_id=1, source_target_pairs={{0,1},{1,2},{2,3},{3,4},{4,5},{5,6},{6,7},{7,8},{8,9},{9,10},{10,1... | collective-permute-start | bytes 983048 | tf_op jit(solution)/shard_map/ppermute | solution.py:768
  46.7 1.3 %copy-start.1 = (s32[2,34]{1,0:T(2,128)S(1)}, s32[2,34]{1,0:T(2,128)}, u32[]{:S(2)}) copy-start(s32[2,34]{1,0:T(2,128)} %constant.5.clone.tab) | copy-start | bytes 820
  46.7 20.1 %collective-permute-start.5 = (f32[640,128]{1,0:T(8,128)S(1)}, f32[640,128]{1,0:T(8,128)S(1)}, u32[]{:S(2)}, u32[]{:S(2)}) collective-permute-start(f32[640,128]{1,0:T(8,128)S(1)} %get-tuple-element.37), channel_id=1, source_target_pairs={{1,0},{2,1},{3,2},{4,3},{5,4},{6,5},{7,6},{8,7},{9,8},{10,9},{11,1... | collective-permute-start | bytes 983048 | tf_op jit(solution)/shard_map/ppermute | solution.py:768
